TPU v7x, 8 devices: a whole 2x2x1 slice. The times are simulated.
8 devices in a mesh: dp: 2 (over z, y), dcp: 4 (over x, core).
Axes of the slice: x: 2, y: 2, z: 1, core: 2. Of those that a mesh axis runs over, the one named last changes fastest.
Arguments:
- q_abs: bfloat16 [256, 64, 576], P('dp', 'dcp'), parts along dimension 0
- latent_cache: bfloat16 [256, 4, 4, 256, 576], P('dp', None, 'dcp'), parts along dimension 0
- ctx_len: int32 [256], P('dp'), parts along dimension 0
Outputs:
- output: bfloat16 [256, 64, 512], P(('dp', 'dcp')), parts along dimension 0
There are 2 independent parts. A program takes and returns all parts, laid end to end along the dimension named above; each array names one.
All inputs are finite; a program needn't handle non-finite values.
Results may differ from a plain program's by a relative error of at most 0.00722076.
Values are sent between devices in bfloat16 or wider.
A program may use at most 1 GiB of HBM per device.

v0:
```python
import jax
import jax.numpy as jnp
from jax import lax
from jax.sharding import PartitionSpec as P

ROPE_DIM = 64
QK_DIM = 192


def solution(mesh):
    group_size = mesh.shape['dcp']

    def local_step(q_blk, cache_blk, len_blk):
        batch_rows = q_blk.shape[0]
        num_pages = cache_blk.shape[1]
        page_len = cache_blk.shape[3]
        latent_dim = q_blk.shape[2] - ROPE_DIM
        out_rows = batch_rows // group_size
        dev_index = lax.axis_index('dcp')
        q_full = lax.all_gather(q_blk, 'dcp', axis=1, tiled=True)
        cache_own = cache_blk[:, :, 0]
        scores = jnp.einsum('bhw,bjtw->bhjt', q_full, cache_own, preferred_element_type=jnp.float32) * (QK_DIM ** -0.5)
        positions = (jnp.arange(num_pages)[:, None] * group_size + dev_index) * page_len + jnp.arange(page_len)[None, :]
        is_valid = positions[None] < len_blk[:, None, None]
        scores = jnp.where(is_valid[:, None], scores, -1e30)
        row_max = jnp.max(scores, axis=(2, 3))
        weights_exp = jnp.exp(scores - row_max[:, :, None, None])
        denom_sum = jnp.sum(weights_exp, axis=(2, 3))
        pv_sum = jnp.einsum('bhjt,bjtw->bhw', weights_exp.astype(jnp.bfloat16), cache_own, preferred_element_type=jnp.float32)
        part_out = (pv_sum[..., :latent_dim] / denom_sum[..., None]).astype(jnp.bfloat16)
        part_lse = row_max + jnp.log(denom_sum)
        recv_out = lax.all_to_all(part_out, 'dcp', 0, 0, tiled=True).reshape(group_size, out_rows, part_out.shape[1], latent_dim)
        recv_lse = lax.all_to_all(part_lse, 'dcp', 0, 0, tiled=True).reshape(group_size, out_rows, part_lse.shape[1])
        total_lse = jax.nn.logsumexp(recv_lse, axis=0)
        merge_weights = jnp.exp(recv_lse - total_lse[None])
        merged = jnp.sum(merge_weights[..., None] * recv_out.astype(jnp.float32), axis=0)
        return merged.astype(jnp.bfloat16)

    return jax.shard_map(local_step, mesh=mesh, in_specs=(P('dp', 'dcp', None), P('dp', None, 'dcp', None, None), P('dp')), out_specs=P(('dp', 'dcp'), None, None), check_vma=False)
```

profile of v0, /device:TPU:1, one launch (start us, length us, event | category | flops | bytes accessed | tf_op | source)
XLA Modules:
  0.0 354.5 jit_solution(13950125027961476311)
XLA Ops:
  6.5 0.0 all-gather.2.cloned.1.call-start
  6.5 4.9 %copy.4 = bf16[128,16,576]{2,1,0:T(8,128)(2,1)} copy(bf16[128,16,576]{0,2,1:T(8,128)(2,1)} %param.3) | data formatting | bytes 4718592 | tf_op args[0]
  11.5 0.0 all-gather.2.cloned.1.call-update
  11.5 0.1 iota_add_fusion
  11.6 0.9 broadcast_compare_fusion
  12.4 69.3 %all-gather.2.cloned.1.call-done = bf16[128,64,576]{2,1,0:T(8,128)(2,1)} async-done(((bf16[128,16,576]{2,1,0:T(8,128)(2,1)}), bf16[128,64,576]{2,1,0:T(8,128)(2,1)}) %all-gather.2.cloned.1.call-update) | async-done | bytes 9437200 | tf_op jit(solution)/shard_map/all_gather | solution.py:20
  81.7 63.3 %fusion.4 = (f32[128,64]{1,0:T(8,128)S(1)}, f32[128,64,4,256]{3,1,2,0:T(8,128)}) fusion(pred[128,4,256]{2,1,0:T(4,128)(4,1)S(1)} %broadcast_compare_fusion, bf16[128,4,1,256,576]{3,4,2,1,0:T(8,128)(2,1)} %param.4, bf16[128,64,576]{2,1,0:T(8,128)(2,1)} %all-gather.2.cloned.1.call-done), kind=kOutput, calls=%fused_computation.6 | convolution fusion | flops 9688834048 | bytes 194150400 | tf_op jit(solution)/shard_map/bhw,bjtw->bhjt/dot_general | solution.py:22
  145.0 69.9 %fusion.15 = f32[128,64,576]{2,1,0:T(8,128)} fusion(bf16[128,4,1,256,576]{3,4,2,1,0:T(8,128)(2,1)} %param.4, f32[128,64,4,256]{3,1,2,0:T(8,128)} %get-tuple-element.6, f32[128,64]{1,0:T(8,128)S(1)} %get-tuple-element.5, pred[128,4,256]{2,1,0:T(4,128)(4,1)S(1)} %broadcast_compare_fusion), kind=kOutput, calls=%fused_computation.18 | convolution fusion | flops 9697230848 | bytes 203587584 | tf_op jit(solution)/shard_map/bhjt,bjtw->bhw/dot_general | solution.py:29
  214.8 14.9 %fusion.6 = f32[128,64]{1,0:T(8,128)S(1)} fusion(f32[128,64,4,256]{3,1,2,0:T(8,128)} %get-tuple-element.6, f32[128,64]{1,0:T(8,128)S(1)} %get-tuple-element.5, pred[128,4,256]{2,1,0:T(4,128)(4,1)S(1)} %broadcast_compare_fusion), kind=kLoop, calls=%fused_computation.8 | loop fusion | flops 33546240 | bytes 33751040 | tf_op jit(solution)/shard_map/reduce_sum | solution.py:28
  229.8 0.7 reshape.62
  230.5 3.5 all-to-all-start
  234.0 9.2 %fusion.8 = bf16[128,64,512]{2,1,0:T(8,128)(2,1)} fusion(f32[128,64,576]{2,1,0:T(8,128)} %fusion.15, f32[128,64]{1,0:T(8,128)S(1)} %fusion.6), kind=kLoop, calls=%fused_computation.10 | loop fusion | flops 8388608 | bytes 25198592 | tf_op jit(solution)/shard_map/convert_element_type | solution.py:30
  243.2 0.0 all-to-all-done
  243.2 5.7 %all-to-all-start.1 = ((bf16[128,64,512]{2,1,0:T(8,128)(2,1)}), bf16[128,64,512]{2,1,0:T(8,128)(2,1)}, u32[]{:S(2)}, u32[]{:S(2)}) async-start(bf16[128,64,512]{2,1,0:T(8,128)(2,1)} %fusion.8), calls=%async_computation.1 | async-start | bytes 16777216 | tf_op jit(solution)/shard_map/all_to_all | solution.py:32
  248.9 0.5 broadcast.56
  249.4 0.7 reduce
  250.1 0.1 reshape.63
  250.3 90.6 %all-to-all-done.1 = bf16[128,64,512]{2,1,0:T(8,128)(2,1)} async-done(((bf16[128,64,512]{2,1,0:T(8,128)(2,1)}), bf16[128,64,512]{2,1,0:T(8,128)(2,1)}, u32[]{:S(2)}, u32[]{:S(2)}) %all-to-all-start.1) | async-done | bytes 8388640 | tf_op jit(solution)/shard_map/all_to_all | solution.py:32
  340.9 6.8 %fusion.9 = bf16[32,64,512]{2,1,0:T(8,128)(2,1)} fusion(bf16[4,32,64,512]{3,2,1,0:T(8,128)(2,1)} %bitcast.8, f32[4,32,64]{2,1,0:T(8,128)S(1)} %subtract_exponential_fusion.1), kind=kLoop, calls=%fused_computation.12 | loop fusion | flops 11534336 | bytes 10518528 | tf_op jit(solution)/shard_map/reduce_sum | solution.py:36
  (7 shorter events, 0.1 us)
Async XLA Ops:
  6.5 75.2 %all-gather.2.cloned.1.call-start = ((), (), s32[]{:S(2)}) async-start(), calls=%async_computation.2 | async-start | bytes 13107200 | tf_op jit(solution)/shard_map/all_gather | solution.py:20
  230.5 12.7 %all-to-all-start = ((f32[4,1,2048]{2,1,0:T(1,128)}), f32[4,1,2048]{2,1,0:T(1,128)S(1)}, u32[]{:S(2)}, u32[]{:S(2)}) async-start(f32[4,1,2048]{2,1,0:T(1,128)} %reshape.62), calls=%async_computation | async-start | bytes 65536 | tf_op jit(solution)/shard_map/all_to_all | solution.py:33
  243.2 97.7 %all-to-all-start.1 = ((bf16[128,64,512]{2,1,0:T(8,128)(2,1)}), bf16[128,64,512]{2,1,0:T(8,128)(2,1)}, u32[]{:S(2)}, u32[]{:S(2)}) async-start(bf16[128,64,512]{2,1,0:T(8,128)(2,1)} %fusion.8), calls=%async_computation.1 | async-start | bytes 16777216 | tf_op jit(solution)/shard_map/all_to_all | solution.py:32
Sparse Core Ops, SparseCore 0:
  11.6 70.0 all-gather.1
where the time goes:
time: 356 us; the launch traced here: 355 us
  waiting for transfers between devices  160 us (45%)
  matrix products  133 us (37%)
  other arithmetic  32.6 us (9%)
  between operations  13.5 us (4%)
  starting transfers between devices  9.19 us (3%)
  local copies, waits for them, and re-layouts  6.24 us (2%)
    all_to_all x1, waiting for transfers between devices, local_step(): lax.all_to_all(part_out, 'dcp', 0, 0, tiled=True)  90.6 us
    dot_general x1, matrix products, local_step(): jnp.einsum('bhjt,bjtw->bhw', weights_exp.astype(jnp.bfloat16), cache_own,...  69.9 us
    all_gather x1, waiting for transfers between devices, local_step(): q_full = lax.all_gather(q_blk, 'dcp', axis=1, tiled=True)  69.3 us
    dot_general x1, matrix products, local_step(): jnp.einsum('bhw,bjtw->bhjt', q_full, cache_own, preferred_element_type=jn...  63.3 us
    reduce_sum x1, other arithmetic, local_step(): denom_sum = jnp.sum(weights_exp, axis=(2, 3))  14.9 us
    convert_element_type x1, other arithmetic, local_step(): (pv_sum[..., :latent_dim] / denom_sum[..., None]).astype(jnp.bfloat16)  9.18 us
  transfers between devices with their start and end apart: 3, of which 2 were waited for; matrix products, arithmetic and copies ran while one was open for 3% of the time, Pallas kernels for 0%

commit v1 on v0

v1 whole, which is shorter than its diff:
```python
import functools
import math

import jax
import jax.numpy as jnp
from jax import lax
from jax.experimental import pallas as pl
from jax.experimental.pallas import tpu as pltpu
from jax.sharding import PartitionSpec as P

ROPE_DIM = 64
QK_DIM = 192
GROUP = 4
CHUNK = 8
PAIR = 2
SLOTS = 3


def attend(q, cache, base, length):
    num_pages, width, page_len = cache.shape
    latent = width - ROPE_DIM
    scores = []
    for j in range(num_pages):
        page = jnp.dot(q, cache[j], preferred_element_type=jnp.float32)
        if j >= num_pages // 2:
            lane = lax.broadcasted_iota(jnp.int32, (1, page_len), 1)
            page = jnp.where(lane < length - (j * GROUP + base) * page_len, page, -jnp.inf)
        scores.append(page)
    top = jnp.max(functools.reduce(jnp.maximum, scores), axis=1, keepdims=True)
    scale = QK_DIM**-0.5
    weights = [jnp.exp2((page - top) * (scale * math.log2(math.e))) for page in scores]
    total = jnp.sum(functools.reduce(jnp.add, weights), axis=1, keepdims=True)
    mixed = functools.reduce(jnp.add, [
        lax.dot_general(weights[j].astype(jnp.bfloat16), cache[j, :latent], (((1,), (1,)), ((), ())),
                        preferred_element_type=jnp.float32) for j in range(num_pages)])
    return (mixed / total).astype(jnp.bfloat16), top * scale + jnp.log(total)


def kernel(q_hbm, cache_hbm, len_ref, out_hbm, q_all, ring, o_buf, o_recv, lse_buf, lse_recv, out_buf,
           own_sem, ring_sem, xs_sem, xr_sem, ds_sem, dr_sem, rs_sem, rr_sem, os_sem, or_sem, ls_sem, lr_sem, out_sem):
    rows, heads, width = q_hbm.shape
    latent = width - ROPE_DIM
    num_chunks = rows // CHUNK
    quarter = num_chunks // GROUP
    steps = rows // PAIR
    per_chunk = CHUNK // PAIR
    me = lax.axis_index("dcp")
    chip = me // 2
    core = me % 2
    across = (me + 2) % GROUP
    sibling = chip * 2 + (1 - core)
    diagonal = (sibling + 2) % GROUP
    first = (1 - chip) * (rows // 2)

    def start_row(k):
        return pl.multiple_of((first + k * CHUNK) % rows, CHUNK)

    def fetch(step):
        row = (first + step * PAIR) % rows
        slot = step % SLOTS
        return pltpu.make_async_copy(cache_hbm.at[pl.ds(row, PAIR), :, 0], ring.at[slot], ring_sem.at[slot])

    def send(src, dst, ssem, rsem, device):
        return pltpu.make_async_remote_copy(src_ref=src, dst_ref=dst, send_sem=ssem, recv_sem=rsem,
                                            device_id={"dcp": device}, device_id_type=pl.DeviceIdType.MESH)

    def send_across(k):
        row = pl.ds(pl.multiple_of((chip * (rows // 2) + k * CHUNK) % rows, CHUNK), CHUNK)
        return send(q_hbm.at[row], q_all.at[me, row], xs_sem.at[k], xr_sem.at[k], across)

    def got_across(k):
        row = pl.ds(start_row(k), CHUNK)
        return send(q_hbm.at[row], q_all.at[across, row], xs_sem.at[k], xr_sem.at[k], across)

    def send_sibling(k):
        row = pl.ds(start_row(k), CHUNK)
        return send(q_hbm.at[row], q_all.at[me, row], ds_sem.at[k], dr_sem.at[k], sibling)

    def got_sibling(k):
        row = pl.ds(start_row(k), CHUNK)
        return send(q_hbm.at[row], q_all.at[sibling, row], ds_sem.at[k], dr_sem.at[k], sibling)

    def relay(k):
        row = pl.ds(start_row(k), CHUNK)
        return send(q_all.at[across, row], q_all.at[across, row], rs_sem.at[k], rr_sem.at[k], sibling)

    def got_relay(k):
        row = pl.ds(start_row(k), CHUNK)
        return send(q_all.at[across, row], q_all.at[diagonal, row], rs_sem.at[k], rr_sem.at[k], sibling)

    def send_part(g, slot, device):
        k = g % quarter
        return (send(o_buf.at[pl.ds(pl.multiple_of(g * CHUNK, CHUNK), CHUNK)], o_recv.at[slot, k],
                     os_sem.at[slot, k], or_sem.at[slot, k], device),
                send(lse_buf.at[g], lse_recv.at[slot, k], ls_sem.at[slot, k], lr_sem.at[slot, k], device))

    own = pltpu.make_async_copy(q_hbm, q_all.at[me], own_sem)
    own.start()
    for step in range(SLOTS - 1):
        fetch(step).start()

    barrier = pltpu.get_barrier_semaphore()
    for device in (across, sibling, diagonal):
        pl.semaphore_signal(barrier, inc=1, device_id={"dcp": device}, device_id_type=pl.DeviceIdType.MESH)
    pl.semaphore_wait(barrier, 3)

    def issue(k, carry):
        send_across(k).start()
        send_sibling(k).start()
        return carry

    lax.fori_loop(0, num_chunks, issue, 0)
    own.wait()
    got_across(0).wait_recv()
    relay(0).start()

    def chunk_step(g, carry):
        @pl.when(g + 1 < num_chunks)
        def _():
            got_across(g + 1).wait_recv()
            relay(g + 1).start()

        got_sibling(g).wait_recv()
        got_relay(g).wait_recv()

        def pair_step(p, lse_acc):
            step = g * per_chunk + p
            fetch(step).wait()

            @pl.when(step + SLOTS - 1 < steps)
            def _():
                fetch(step + SLOTS - 1).start()

            slot = step % SLOTS
            for i in range(PAIR):
                row = (first + step * PAIR + i) % rows
                q = jnp.concatenate([q_all[d, row] for d in range(GROUP)], axis=0)
                o, lse = attend(q, ring[slot, i], me, len_ref[row])
                o_buf[step * PAIR + i] = o
                lane = lax.broadcasted_iota(jnp.int32, lse_acc.shape, 1)
                lse_acc = jnp.where(lane == p * PAIR + i, lse, lse_acc)
            return lse_acc

        lse_acc = lax.fori_loop(0, per_chunk, pair_step, jnp.zeros((GROUP * heads, 128), jnp.float32))
        padded = jnp.concatenate([lse_acc, jnp.zeros((128 - GROUP * heads, 128), jnp.float32)], axis=0)
        lse_buf[g] = padded.T[:CHUNK]

        @pl.when(g < 2 * quarter)
        def _():
            target = (1 - chip) * 2 + g // quarter
            for copy in send_part(g, 1 + (g // quarter + core) % 2, target):
                copy.start()

        @pl.when((g >= 2 * quarter) & (g // quarter - 2 != core))
        def _():
            for copy in send_part(g, 0, sibling):
                copy.start()

        return carry

    lax.fori_loop(0, num_chunks, chunk_step, 0)

    own_first = (2 + core) * quarter

    def merge_step(k, carry):
        for slot in range(GROUP - 1):
            for copy in send_part(k, slot, sibling):
                copy.wait_recv()
        lses = [lse_buf[own_first + k]] + [lse_recv[slot, k] for slot in range(GROUP - 1)]
        top = functools.reduce(jnp.maximum, lses)
        total = top + jnp.log(functools.reduce(jnp.add, [jnp.exp(x - top) for x in lses]))
        factors = jnp.concatenate([jnp.exp(x - total) for x in lses], axis=0)
        padded = jnp.concatenate([factors, jnp.zeros((128 - GROUP * CHUNK, 128), jnp.float32)], axis=0)
        columns = padded.T[:GROUP * heads]
        for i in range(CHUNK):
            parts = [o_buf[(own_first + k) * CHUNK + i]] + [o_recv[slot, k, i] for slot in range(GROUP - 1)]
            merged = functools.reduce(
                jnp.add, [columns[:, s * CHUNK + i:s * CHUNK + i + 1] * part.astype(jnp.float32) for s, part in enumerate(parts)])
            out_buf[k * CHUNK + i] = merged.astype(jnp.bfloat16)
        row = pl.ds(pl.multiple_of(k * CHUNK, CHUNK), CHUNK)
        pltpu.make_async_copy(out_buf.at[row], out_hbm.at[row], out_sem.at[k]).start()
        return carry

    lax.fori_loop(0, quarter, merge_step, 0)

    def drain(k, carry):
        send_across(k).wait_send()
        send_sibling(k).wait_send()
        relay(k).wait_send()
        return carry

    lax.fori_loop(0, num_chunks, drain, 0)
    for k in range(quarter):
        for slot in range(GROUP - 1):
            for copy in send_part(k, slot, sibling):
                copy.wait_send()
        row = pl.ds(k * CHUNK, CHUNK)
        pltpu.make_async_copy(out_buf.at[row], out_hbm.at[row], out_sem.at[k]).wait()


def solution(mesh):
    def local_step(q_blk, cache_blk, len_blk):
        rows, heads, width = q_blk.shape
        num_pages, page_len = cache_blk.shape[1], cache_blk.shape[3]
        cache_blk = jnp.swapaxes(cache_blk, 3, 4)
        latent = width - ROPE_DIM
        num_chunks = rows // CHUNK
        quarter = num_chunks // GROUP
        dma = pltpu.SemaphoreType.DMA
        return pl.pallas_call(
            kernel,
            out_shape=jax.ShapeDtypeStruct((rows // GROUP, GROUP * heads, latent), jnp.bfloat16),
            in_specs=[pl.BlockSpec(memory_space=pl.ANY), pl.BlockSpec(memory_space=pl.ANY),
                      pl.BlockSpec(memory_space=pltpu.SMEM)],
            out_specs=pl.BlockSpec(memory_space=pl.ANY),
            scratch_shapes=[
                pltpu.VMEM((GROUP, rows, heads, width), jnp.bfloat16),
                pltpu.VMEM((SLOTS, PAIR, num_pages, width, page_len), jnp.bfloat16),
                pltpu.VMEM((rows, GROUP * heads, latent), jnp.bfloat16),
                pltpu.VMEM((GROUP - 1, quarter, CHUNK, GROUP * heads, latent), jnp.bfloat16),
                pltpu.VMEM((num_chunks, CHUNK, 128), jnp.float32),
                pltpu.VMEM((GROUP - 1, quarter, CHUNK, 128), jnp.float32),
                pltpu.VMEM((rows // GROUP, GROUP * heads, latent), jnp.bfloat16),
                dma(()), dma((SLOTS,)),
                dma((num_chunks,)), dma((num_chunks,)), dma((num_chunks,)), dma((num_chunks,)),
                dma((num_chunks,)), dma((num_chunks,)),
                dma((GROUP - 1, quarter)), dma((GROUP - 1, quarter)),
                dma((GROUP - 1, quarter)), dma((GROUP - 1, quarter)),
                dma((quarter,)),
            ],
            compiler_params=pltpu.CompilerParams(collective_id=0, has_side_effects=True, vmem_limit_bytes=60 * 2**20),
        )(q_blk, cache_blk, len_blk)

    return jax.shard_map(local_step, mesh=mesh, in_specs=(P('dp', 'dcp', None), P('dp', None, 'dcp', None, None), P('dp')), out_specs=P(('dp', 'dcp'), None, None), check_vma=False)
```

time: 356 us -> 162 us (0.46)
  waiting for transfers between devices: 160 us -> 0 us
  Pallas kernels: 0 us -> 154 us
  matrix products: 133 us -> 0 us
  other arithmetic: 32.6 us -> 0 us
  between operations: 13.5 us -> 0.01 us
  starting transfers between devices: 9.19 us -> 0 us
    pallas_call x0 -> x1, Pallas kernels: none -> 154 us  [local_step(): pl.pallas_call(kernel, out_shape=jax.ShapeDtypeStruct((rows // GROUP, GRO...]
    dot_general x2 -> x0, matrix products: 133 us -> none  [the longest x1 69.9 us: local_step(): jnp.einsum('bhjt,bjtw->bhw', weights_exp.astype(jnp.bfloat16), cache_own,...]
    all_to_all x2 -> x0, waiting for transfers between devices: 90.6 us -> none  [the longest x1 90.6 us: local_step(): lax.all_to_all(part_out, 'dcp', 0, 0, tiled=True)]
    all_gather x1 -> x0, waiting for transfers between devices: 69.3 us -> none  [local_step(): q_full = lax.all_gather(q_blk, 'dcp', axis=1, tiled=True)]
    reduce_sum x3 -> x0, other arithmetic: 21.7 us -> none  [the longest x1 14.9 us: local_step(): denom_sum = jnp.sum(weights_exp, axis=(2, 3))]
    all_to_all x2 -> x0, starting transfers between devices: 9.19 us -> none  [the longest x1 5.7 us: local_step(): lax.all_to_all(part_out, 'dcp', 0, 0, tiled=True)]
    convert_element_type x1 -> x0, other arithmetic: 9.18 us -> none  [local_step(): (pv_sum[..., :latent_dim] / denom_sum[..., None]).astype(jnp.bfloat16)]
    unnamed x3 -> x2, local copies, waits for them, and re-layouts: 5.73 us -> 8.04 us
  transfers between devices with their start and end apart: 3 -> 0, of which waited for: 2 -> 0; matrix products, arithmetic and copies ran while one was open for 3% -> 0% of each run, Pallas kernels for 0% -> 0%
where the time goes in v1:
time: 162 us
  Pallas kernels  154 us (95%)
  local copies, waits for them, and re-layouts  8.04 us (5%)
    pallas_call x1, Pallas kernels, local_step(): pl.pallas_call(kernel, out_shape=jax.ShapeDtypeStruct((rows // GROUP, GRO...  154 us
    unnamed x2, local copies, waits for them, and re-layouts  8.04 us

profile of v1, /device:TPU:1, one launch (start us, length us, event | category | flops | bytes accessed | tf_op | source)
XLA Modules:
  0.0 161.9 jit_solution(10686897743184356630)
XLA Ops:
  0.0 4.9 %copy.4.q_hbm = bf16[128,16,576]{2,1,0:T(8,128)(2,1)} copy(bf16[128,16,576]{0,2,1:T(8,128)(2,1)} %param.3) | data formatting | bytes 4718592 | tf_op args[0]
  4.9 153.8 %shard_map.37 = bf16[32,64,512]{2,1,0:T(8,128)(2,1)} custom-call(bf16[128,16,576]{2,1,0:T(8,128)(2,1)} %copy.4.q_hbm, bf16[128,4,1,576,256]{4,3,2,1,0:T(8,128)(2,1)} %bitcast.cache_hbm, s32[128]{0:T(128)} %len_ref.1), custom_call_target="tpu_custom_call" | custom-call | tf_op jit(solution)/shard_map/pallas_call | solution.py:210
  158.8 3.1 %copy.6 = bf16[32,64,512]{2,1,0:T(8,128)(2,1)} copy(bf16[32,64,512]{2,1,0:T(8,128)(2,1)} %shard_map.37) | data formatting | bytes 4194304

commit v2 on v1

--- a/solution.py
+++ b/solution.py
@@ -16,12 +16,13 @@
 SLOTS = 3
 
 
-def attend(q, cache, base, length):
+def attend(q, q_rope, cache, base, length):
     num_pages, width, page_len = cache.shape
     latent = width - ROPE_DIM
     scores = []
     for j in range(num_pages):
-        page = jnp.dot(q, cache[j], preferred_element_type=jnp.float32)
+        page = (jnp.dot(q, cache[j, :latent], preferred_element_type=jnp.float32)
+                + jnp.dot(q_rope, cache[j, latent:], preferred_element_type=jnp.float32))
         if j >= num_pages // 2:
             lane = lax.broadcasted_iota(jnp.int32, (1, page_len), 1)
             page = jnp.where(lane < length - (j * GROUP + base) * page_len, page, -jnp.inf)
@@ -36,9 +37,9 @@
     return (mixed / total).astype(jnp.bfloat16), top * scale + jnp.log(total)
 
 
-def kernel(q_hbm, cache_hbm, len_ref, out_hbm, q_all, ring, o_buf, o_recv, lse_buf, lse_recv, out_buf,
-           own_sem, ring_sem, xs_sem, xr_sem, ds_sem, dr_sem, rs_sem, rr_sem, os_sem, or_sem, ls_sem, lr_sem, out_sem):
-    rows, heads, width = q_hbm.shape
+def kernel(q_hbm, cache_hbm, len_ref, out_hbm, q_raw, q_turned, q_all, rope_raw, rope_turned, rope_all, ring, o_buf, o_recv, lse_buf, lse_recv, out_buf,
+           own_sem, ps_sem, pr_sem, ring_sem, xs_sem, xr_sem, ds_sem, dr_sem, rs_sem, rr_sem, os_sem, or_sem, ls_sem, lr_sem, out_sem):
+    heads, width, rows = q_hbm.shape
     latent = width - ROPE_DIM
     num_chunks = rows // CHUNK
     quarter = num_chunks // GROUP
@@ -66,19 +67,19 @@
 
     def send_across(k):
         row = pl.ds(pl.multiple_of((chip * (rows // 2) + k * CHUNK) % rows, CHUNK), CHUNK)
-        return send(q_hbm.at[row], q_all.at[me, row], xs_sem.at[k], xr_sem.at[k], across)
+        return send(q_all.at[me, row], q_all.at[me, row], xs_sem.at[k], xr_sem.at[k], across)
 
     def got_across(k):
         row = pl.ds(start_row(k), CHUNK)
-        return send(q_hbm.at[row], q_all.at[across, row], xs_sem.at[k], xr_sem.at[k], across)
+        return send(q_all.at[me, row], q_all.at[across, row], xs_sem.at[k], xr_sem.at[k], across)
 
     def send_sibling(k):
         row = pl.ds(start_row(k), CHUNK)
-        return send(q_hbm.at[row], q_all.at[me, row], ds_sem.at[k], dr_sem.at[k], sibling)
+        return send(q_all.at[me, row], q_all.at[me, row], ds_sem.at[k], dr_sem.at[k], sibling)
 
     def got_sibling(k):
         row = pl.ds(start_row(k), CHUNK)
-        return send(q_hbm.at[row], q_all.at[sibling, row], ds_sem.at[k], dr_sem.at[k], sibling)
+        return send(q_all.at[me, row], q_all.at[sibling, row], ds_sem.at[k], dr_sem.at[k], sibling)
 
     def relay(k):
         row = pl.ds(start_row(k), CHUNK)
@@ -94,8 +95,14 @@
                      os_sem.at[slot, k], or_sem.at[slot, k], device),
                 send(lse_buf.at[g], lse_recv.at[slot, k], ls_sem.at[slot, k], lr_sem.at[slot, k], device))
 
-    own = pltpu.make_async_copy(q_hbm, q_all.at[me], own_sem)
-    own.start()
+    def send_rope(i, src, dst, device):
+        return send(src, rope_raw.at[dst], ps_sem.at[i], pr_sem.at[i], device)
+
+    own_rope = q_hbm.at[:, pl.ds(latent, ROPE_DIM), :]
+    own = [pltpu.make_async_copy(q_hbm.at[:, pl.ds(0, latent), :], q_raw, own_sem.at[0]),
+           pltpu.make_async_copy(own_rope, rope_raw.at[me], own_sem.at[1])]
+    for copy in own:
+        copy.start()
     for step in range(SLOTS - 1):
         fetch(step).start()
 
@@ -104,13 +111,58 @@
         pl.semaphore_signal(barrier, inc=1, device_id={"dcp": device}, device_id_type=pl.DeviceIdType.MESH)
     pl.semaphore_wait(barrier, 3)
 
+    send_rope(0, own_rope, me, across).start()
+    send_rope(1, own_rope, me, sibling).start()
+
+    block = heads * heads
+    into = lax.broadcasted_iota(jnp.int32, (block, block), 0)
+    out_of = lax.broadcasted_iota(jnp.int32, (block, block), 1)
+    swap = jnp.where(out_of == (into % heads) * heads + into // heads, 1.0, 0.0).astype(jnp.bfloat16)
+
+    def interleave(turned, i):
+        part = turned[:, pl.ds(pl.multiple_of(i * heads, heads), heads), :]
+        lanes = part.shape[2]
+        mixed = jnp.dot(swap, part.reshape(block, lanes), preferred_element_type=jnp.float32)
+        return mixed.astype(jnp.bfloat16).reshape(heads, heads, lanes)
+
+    own[0].wait()
+
+    def turn(h, carry):
+        q_turned[h] = q_raw[h].T
+        return carry
+
+    lax.fori_loop(0, heads, turn, 0)
+
+    def place(i, carry):
+        q_all[me, pl.ds(pl.multiple_of(i * heads, heads), heads)] = interleave(q_turned, i)
+        return carry
+
+    lax.fori_loop(0, rows // heads, place, 0)
+
     def issue(k, carry):
         send_across(k).start()
         send_sibling(k).start()
         return carry
 
     lax.fori_loop(0, num_chunks, issue, 0)
-    own.wait()
+    send_rope(0, own_rope, across, across).wait_recv()
+    send_rope(2, rope_raw.at[across], across, sibling).start()
+    own[1].wait()
+    send_rope(1, own_rope, sibling, sibling).wait_recv()
+    send_rope(2, rope_raw.at[across], diagonal, sibling).wait_recv()
+
+    def turn_rope(h, carry):
+        rope_turned[h] = jnp.concatenate(
+            [jnp.concatenate([rope_raw[d, h], rope_raw[d + 1, h]], axis=0).T for d in range(0, GROUP, 2)], axis=1)
+        return carry
+
+    lax.fori_loop(0, heads, turn_rope, 0)
+
+    def place_rope(i, carry):
+        rope_all[pl.ds(pl.multiple_of(i * heads, heads), heads)] = interleave(rope_turned, i)
+        return carry
+
+    lax.fori_loop(0, rows // heads, place_rope, 0)
     got_across(0).wait_recv()
     relay(0).start()
 
@@ -135,7 +187,9 @@
             for i in range(PAIR):
                 row = (first + step * PAIR + i) % rows
                 q = jnp.concatenate([q_all[d, row] for d in range(GROUP)], axis=0)
-                o, lse = attend(q, ring[slot, i], me, len_ref[row])
+                rope = rope_all[row]
+                q_rope = jnp.concatenate([rope[:, d * ROPE_DIM:(d + 1) * ROPE_DIM] for d in range(GROUP)], axis=0)
+                o, lse = attend(q, q_rope, ring[slot, i], me, len_ref[row])
                 o_buf[step * PAIR + i] = o
                 lane = lax.broadcasted_iota(jnp.int32, lse_acc.shape, 1)
                 lse_acc = jnp.where(lane == p * PAIR + i, lse, lse_acc)
@@ -190,6 +244,9 @@
         return carry
 
     lax.fori_loop(0, num_chunks, drain, 0)
+    send_rope(0, own_rope, me, across).wait_send()
+    send_rope(1, own_rope, me, sibling).wait_send()
+    send_rope(2, rope_raw.at[across], across, sibling).wait_send()
     for k in range(quarter):
         for slot in range(GROUP - 1):
             for copy in send_part(k, slot, sibling):
@@ -206,6 +263,7 @@
         latent = width - ROPE_DIM
         num_chunks = rows // CHUNK
         quarter = num_chunks // GROUP
+        q_blk = jnp.transpose(q_blk, (1, 2, 0))
         dma = pltpu.SemaphoreType.DMA
         return pl.pallas_call(
             kernel,
@@ -214,14 +272,19 @@
                       pl.BlockSpec(memory_space=pltpu.SMEM)],
             out_specs=pl.BlockSpec(memory_space=pl.ANY),
             scratch_shapes=[
-                pltpu.VMEM((GROUP, rows, heads, width), jnp.bfloat16),
+                pltpu.VMEM((heads, latent, rows), jnp.bfloat16),
+                pltpu.VMEM((heads, rows, latent), jnp.bfloat16),
+                pltpu.VMEM((GROUP, rows, heads, latent), jnp.bfloat16),
+                pltpu.VMEM((GROUP, heads, ROPE_DIM, rows), jnp.bfloat16),
+                pltpu.VMEM((heads, rows, GROUP * ROPE_DIM), jnp.bfloat16),
+                pltpu.VMEM((rows, heads, GROUP * ROPE_DIM), jnp.bfloat16),
                 pltpu.VMEM((SLOTS, PAIR, num_pages, width, page_len), jnp.bfloat16),
                 pltpu.VMEM((rows, GROUP * heads, latent), jnp.bfloat16),
                 pltpu.VMEM((GROUP - 1, quarter, CHUNK, GROUP * heads, latent), jnp.bfloat16),
                 pltpu.VMEM((num_chunks, CHUNK, 128), jnp.float32),
                 pltpu.VMEM((GROUP - 1, quarter, CHUNK, 128), jnp.float32),
                 pltpu.VMEM((rows // GROUP, GROUP * heads, latent), jnp.bfloat16),
-                dma(()), dma((SLOTS,)),
+                dma((2,)), dma((3,)), dma((3,)), dma((SLOTS,)),
                 dma((num_chunks,)), dma((num_chunks,)), dma((num_chunks,)), dma((num_chunks,)),
                 dma((num_chunks,)), dma((num_chunks,)),
                 dma((GROUP - 1, quarter)), dma((GROUP - 1, quarter)),

time: 162 us -> 152 us (0.938)
  Pallas kernels: 154 us -> 148 us
  local copies, waits for them, and re-layouts: 8.04 us -> 3.13 us
    pallas_call x1, Pallas kernels: 154 us -> 148 us  [local_step(): pl.pallas_call(kernel, out_shape=jax.ShapeDtypeStruct((rows // GROUP, GRO...]
    unnamed x2 -> x1, local copies, waits for them, and re-layouts: 8.04 us -> 3.13 us
where the time goes in v2:
time: 152 us; the launch traced here: 151 us
  Pallas kernels  148 us (97%)
  local copies, waits for them, and re-layouts  3.13 us (2%)
    pallas_call x1, Pallas kernels, local_step(): pl.pallas_call(kernel, out_shape=jax.ShapeDtypeStruct((rows // GROUP, GRO...  148 us
    unnamed x1, local copies, waits for them, and re-layouts  3.13 us

profile of v2, /device:TPU:1, one launch (start us, length us, event | category | flops | bytes accessed | tf_op | source)
XLA Modules:
  0.0 151.5 jit_solution(3452190848611500249)
XLA Ops:
  0.0 148.3 %shard_map.37 = bf16[32,64,512]{2,1,0:T(8,128)(2,1)} custom-call(bf16[16,576,128]{2,1,0:T(8,128)(2,1)} %bitcast.2, bf16[128,4,1,576,256]{4,3,2,1,0:T(8,128)(2,1)} %bitcast.1.cache_hbm, s32[128]{0:T(128)} %len_ref.1), custom_call_target="tpu_custom_call" | custom-call | tf_op jit(solution)/shard_map/pallas_call | solution.py:268
  148.3 3.1 %copy.5 = bf16[32,64,512]{2,1,0:T(8,128)(2,1)} copy(bf16[32,64,512]{2,1,0:T(8,128)(2,1)} %shard_map.37) | data formatting | bytes 4194304

commit v3 on v2

--- a/solution.py
+++ b/solution.py
@@ -12,6 +12,7 @@
 QK_DIM = 192
 GROUP = 4
 CHUNK = 8
+PIECE = 4
 PAIR = 2
 SLOTS = 3
 
@@ -37,8 +38,8 @@
     return (mixed / total).astype(jnp.bfloat16), top * scale + jnp.log(total)
 
 
-def kernel(q_hbm, cache_hbm, len_ref, out_hbm, q_raw, q_turned, q_all, rope_raw, rope_turned, rope_all, ring, o_buf, o_recv, lse_buf, lse_recv, out_buf,
-           own_sem, ps_sem, pr_sem, ring_sem, xs_sem, xr_sem, ds_sem, dr_sem, rs_sem, rr_sem, os_sem, or_sem, ls_sem, lr_sem, out_sem):
+def kernel(q_hbm, cache_hbm, len_ref, out_ref, q_raw, q_turned, q_all, rope_raw, rope_turned, rope_all, ring, o_buf, o_recv, lse_buf, lse_recv,
+           own_sem, ps_sem, pr_sem, ring_sem, xs_sem, xr_sem, ds_sem, dr_sem, rs_sem, rr_sem, os_sem, or_sem, ls_sem, lr_sem):
     heads, width, rows = q_hbm.shape
     latent = width - ROPE_DIM
     num_chunks = rows // CHUNK
@@ -91,9 +92,12 @@
 
     def send_part(g, slot, device):
         k = g % quarter
-        return (send(o_buf.at[pl.ds(pl.multiple_of(g * CHUNK, CHUNK), CHUNK)], o_recv.at[slot, k],
-                     os_sem.at[slot, k], or_sem.at[slot, k], device),
-                send(lse_buf.at[g], lse_recv.at[slot, k], ls_sem.at[slot, k], lr_sem.at[slot, k], device))
+        copies = [send(lse_buf.at[g], lse_recv.at[slot, k], ls_sem.at[slot, k], lr_sem.at[slot, k], device)]
+        for i in range(CHUNK // PIECE):
+            rows_i = pl.ds(pl.multiple_of(g * CHUNK + i * PIECE, PIECE), PIECE)
+            copies.append(send(o_buf.at[rows_i], o_recv.at[slot, k, pl.ds(i * PIECE, PIECE)],
+                               os_sem.at[slot, k, i], or_sem.at[slot, k, i], device))
+        return copies
 
     def send_rope(i, src, dst, device):
         return send(src, rope_raw.at[dst], ps_sem.at[i], pr_sem.at[i], device)
@@ -217,9 +221,9 @@
     own_first = (2 + core) * quarter
 
     def merge_step(k, carry):
-        for slot in range(GROUP - 1):
-            for copy in send_part(k, slot, sibling):
-                copy.wait_recv()
+        parts_of = [send_part(k, slot, sibling) for slot in range(GROUP - 1)]
+        for part in parts_of:
+            part[0].wait_recv()
         lses = [lse_buf[own_first + k]] + [lse_recv[slot, k] for slot in range(GROUP - 1)]
         top = functools.reduce(jnp.maximum, lses)
         total = top + jnp.log(functools.reduce(jnp.add, [jnp.exp(x - top) for x in lses]))
@@ -227,12 +231,13 @@
         padded = jnp.concatenate([factors, jnp.zeros((128 - GROUP * CHUNK, 128), jnp.float32)], axis=0)
         columns = padded.T[:GROUP * heads]
         for i in range(CHUNK):
+            if i % PIECE == 0:
+                for part in parts_of:
+                    part[1 + i // PIECE].wait_recv()
             parts = [o_buf[(own_first + k) * CHUNK + i]] + [o_recv[slot, k, i] for slot in range(GROUP - 1)]
             merged = functools.reduce(
                 jnp.add, [columns[:, s * CHUNK + i:s * CHUNK + i + 1] * part.astype(jnp.float32) for s, part in enumerate(parts)])
-            out_buf[k * CHUNK + i] = merged.astype(jnp.bfloat16)
-        row = pl.ds(pl.multiple_of(k * CHUNK, CHUNK), CHUNK)
-        pltpu.make_async_copy(out_buf.at[row], out_hbm.at[row], out_sem.at[k]).start()
+            out_ref[k * CHUNK + i] = merged.astype(jnp.bfloat16)
         return carry
 
     lax.fori_loop(0, quarter, merge_step, 0)
@@ -251,8 +256,6 @@
         for slot in range(GROUP - 1):
             for copy in send_part(k, slot, sibling):
                 copy.wait_send()
-        row = pl.ds(k * CHUNK, CHUNK)
-        pltpu.make_async_copy(out_buf.at[row], out_hbm.at[row], out_sem.at[k]).wait()
 
 
 def solution(mesh):
@@ -267,10 +270,10 @@
         dma = pltpu.SemaphoreType.DMA
         return pl.pallas_call(
             kernel,
-            out_shape=jax.ShapeDtypeStruct((rows // GROUP, GROUP * heads, latent), jnp.bfloat16),
+            out_shape=pltpu.VMEM((rows // GROUP, GROUP * heads, latent), jnp.bfloat16),
             in_specs=[pl.BlockSpec(memory_space=pl.ANY), pl.BlockSpec(memory_space=pl.ANY),
                       pl.BlockSpec(memory_space=pltpu.SMEM)],
-            out_specs=pl.BlockSpec(memory_space=pl.ANY),
+            out_specs=pl.BlockSpec(memory_space=pltpu.VMEM),
             scratch_shapes=[
                 pltpu.VMEM((heads, latent, rows), jnp.bfloat16),
                 pltpu.VMEM((heads, rows, latent), jnp.bfloat16),
@@ -283,13 +286,11 @@
                 pltpu.VMEM((GROUP - 1, quarter, CHUNK, GROUP * heads, latent), jnp.bfloat16),
                 pltpu.VMEM((num_chunks, CHUNK, 128), jnp.float32),
                 pltpu.VMEM((GROUP - 1, quarter, CHUNK, 128), jnp.float32),
-                pltpu.VMEM((rows // GROUP, GROUP * heads, latent), jnp.bfloat16),
                 dma((2,)), dma((3,)), dma((3,)), dma((SLOTS,)),
                 dma((num_chunks,)), dma((num_chunks,)), dma((num_chunks,)), dma((num_chunks,)),
                 dma((num_chunks,)), dma((num_chunks,)),
+                dma((GROUP - 1, quarter, CHUNK // PIECE)), dma((GROUP - 1, quarter, CHUNK // PIECE)),
                 dma((GROUP - 1, quarter)), dma((GROUP - 1, quarter)),
-                dma((GROUP - 1, quarter)), dma((GROUP - 1, quarter)),
-                dma((quarter,)),
             ],
             compiler_params=pltpu.CompilerParams(collective_id=0, has_side_effects=True, vmem_limit_bytes=60 * 2**20),
         )(q_blk, cache_blk, len_blk)

time: 152 us -> 149 us (0.980)
  local copies, waits for them, and re-layouts: 3.13 us -> 1.32 us
    unnamed x1, local copies, waits for them, and re-layouts: 3.13 us -> 1.32 us
where the time goes in v3:
time: 149 us
  Pallas kernels  148 us (99%)
    pallas_call x1, Pallas kernels, local_step(): pl.pallas_call(kernel, out_shape=pltpu.VMEM((rows // GROUP, GROUP * heads...  148 us

profile of v3, /device:TPU:1, one launch (start us, length us, event | category | flops | bytes accessed | tf_op | source)
XLA Modules:
  0.0 148.9 jit_solution(5259393067170585978)
XLA Ops:
  0.0 147.6 %shard_map.37 = bf16[32,64,512]{2,1,0:T(8,128)(2,1)S(1)} custom-call(bf16[16,576,128]{2,1,0:T(8,128)(2,1)} %bitcast.2, bf16[128,4,1,576,256]{4,3,2,1,0:T(8,128)(2,1)} %bitcast.1.cache_hbm, s32[128]{0:T(128)} %len_ref.1), custom_call_target="tpu_custom_call" | custom-call | tf_op jit(solution)/shard_map/pallas_call | solution.py:271
  147.6 1.3 copy.5

commit v4 on v3

--- a/solution.py
+++ b/solution.py
@@ -39,7 +39,7 @@
 
 
 def kernel(q_hbm, cache_hbm, len_ref, out_ref, q_raw, q_turned, q_all, rope_raw, rope_turned, rope_all, ring, o_buf, o_recv, lse_buf, lse_recv,
-           own_sem, ps_sem, pr_sem, ring_sem, xs_sem, xr_sem, ds_sem, dr_sem, rs_sem, rr_sem, os_sem, or_sem, ls_sem, lr_sem):
+           own_sem, ps_sem, pr_sem, ring_sem, xs_sem, xr_sem, ds_sem, dr_sem, rs_sem, rr_sem, os_sem, or_sem, ls_sem, lr_sem, ready):
     heads, width, rows = q_hbm.shape
     latent = width - ROPE_DIM
     num_chunks = rows // CHUNK
@@ -110,13 +110,24 @@
     for step in range(SLOTS - 1):
         fetch(step).start()
 
+    def tell(semaphore, device):
+        pl.semaphore_signal(semaphore, inc=1, device_id={"dcp": device}, device_id_type=pl.DeviceIdType.MESH)
+
     barrier = pltpu.get_barrier_semaphore()
-    for device in (across, sibling, diagonal):
-        pl.semaphore_signal(barrier, inc=1, device_id={"dcp": device}, device_id_type=pl.DeviceIdType.MESH)
-    pl.semaphore_wait(barrier, 3)
+    tell(barrier, across)
+    pl.semaphore_wait(barrier, 3 - 2 * core)
+
+    @pl.when(core == 1)
+    def _():
+        tell(barrier, sibling)
+        tell(barrier, diagonal)
+
+    @pl.when(core == 0)
+    def _():
+        tell(ready, sibling)
+        tell(ready, diagonal)
 
     send_rope(0, own_rope, me, across).start()
-    send_rope(1, own_rope, me, sibling).start()
 
     block = heads * heads
     into = lax.broadcasted_iota(jnp.int32, (block, block), 0)
@@ -143,12 +154,23 @@
 
     lax.fori_loop(0, rows // heads, place, 0)
 
-    def issue(k, carry):
+    def issue_across(k, carry):
         send_across(k).start()
+        return carry
+
+    lax.fori_loop(0, num_chunks, issue_across, 0)
+
+    @pl.when(core == 1)
+    def _():
+        pl.semaphore_wait(ready, 2)
+
+    send_rope(1, own_rope, me, sibling).start()
+
+    def issue_sibling(k, carry):
         send_sibling(k).start()
         return carry
 
-    lax.fori_loop(0, num_chunks, issue, 0)
+    lax.fori_loop(0, num_chunks, issue_sibling, 0)
     send_rope(0, own_rope, across, across).wait_recv()
     send_rope(2, rope_raw.at[across], across, sibling).start()
     own[1].wait()
@@ -291,6 +313,7 @@
                 dma((num_chunks,)), dma((num_chunks,)),
                 dma((GROUP - 1, quarter, CHUNK // PIECE)), dma((GROUP - 1, quarter, CHUNK // PIECE)),
                 dma((GROUP - 1, quarter)), dma((GROUP - 1, quarter)),
+                pltpu.SemaphoreType.REGULAR,
             ],
             compiler_params=pltpu.CompilerParams(collective_id=0, has_side_effects=True, vmem_limit_bytes=60 * 2**20),
         )(q_blk, cache_blk, len_blk)

time: 149 us -> 148 us (level)
  no operation moved by 1% of the time
where the time goes in v4:
time: 148 us
  Pallas kernels  147 us (99%)
    pallas_call x1, Pallas kernels, local_step(): pl.pallas_call(kernel, out_shape=pltpu.VMEM((rows // GROUP, GROUP * heads...  147 us

profile of v4, /device:TPU:1, one launch (start us, length us, event | category | flops | bytes accessed | tf_op | source)
XLA Modules:
  0.0 148.2 jit_solution(15575789602116646058)
XLA Ops:
  0.0 146.9 %shard_map.37 = bf16[32,64,512]{2,1,0:T(8,128)(2,1)S(1)} custom-call(bf16[16,576,128]{2,1,0:T(8,128)(2,1)} %bitcast.2, bf16[128,4,1,576,256]{4,3,2,1,0:T(8,128)(2,1)} %bitcast.1.cache_hbm, s32[128]{0:T(128)} %len_ref.1), custom_call_target="tpu_custom_call" | custom-call | tf_op jit(solution)/shard_map/pallas_call | solution.py:293
  146.9 1.3 copy.5

commit v5 on v4

--- a/solution.py
+++ b/solution.py
@@ -11,8 +11,8 @@
 ROPE_DIM = 64
 QK_DIM = 192
 GROUP = 4
-CHUNK = 8
-PIECE = 4
+CHUNK = 16
+PIECES = (8, 4, 2, 2)
 PAIR = 2
 SLOTS = 3
 
@@ -38,8 +38,8 @@
     return (mixed / total).astype(jnp.bfloat16), top * scale + jnp.log(total)
 
 
-def kernel(q_hbm, cache_hbm, len_ref, out_ref, q_raw, q_turned, q_all, rope_raw, rope_turned, rope_all, ring, o_buf, o_recv, lse_buf, lse_recv,
-           own_sem, ps_sem, pr_sem, ring_sem, xs_sem, xr_sem, ds_sem, dr_sem, rs_sem, rr_sem, os_sem, or_sem, ls_sem, lr_sem, ready):
+def kernel(q_hbm, cache_hbm, len_hbm, out_ref, len_ref, q_raw, q_turned, q_all, rope_raw, rope_turned, rope_all, ring, o_buf, o_recv, lse_buf, lse_recv,
+           len_sem, own_sem, ps_sem, pr_sem, ring_sem, xs_sem, xr_sem, ds_sem, dr_sem, rs_sem, rr_sem, os_sem, or_sem, ls_sem, lr_sem, ready):
     heads, width, rows = q_hbm.shape
     latent = width - ROPE_DIM
     num_chunks = rows // CHUNK
@@ -92,12 +92,13 @@
 
     def send_part(g, slot, device):
         k = g % quarter
-        copies = [send(lse_buf.at[g], lse_recv.at[slot, k], ls_sem.at[slot, k], lr_sem.at[slot, k], device)]
-        for i in range(CHUNK // PIECE):
-            rows_i = pl.ds(pl.multiple_of(g * CHUNK + i * PIECE, PIECE), PIECE)
-            copies.append(send(o_buf.at[rows_i], o_recv.at[slot, k, pl.ds(i * PIECE, PIECE)],
+        copies, begin = [], 0
+        for i, size in enumerate(PIECES):
+            src = o_buf.at[pl.ds(pl.multiple_of(g * CHUNK + begin, size), size)]
+            copies.append(send(src, o_recv.at[slot, k, pl.ds(begin, size)],
                                os_sem.at[slot, k, i], or_sem.at[slot, k, i], device))
-        return copies
+            begin += size
+        return copies + [send(lse_buf.at[g], lse_recv.at[slot, k], ls_sem.at[slot, k], lr_sem.at[slot, k], device)]
 
     def send_rope(i, src, dst, device):
         return send(src, rope_raw.at[dst], ps_sem.at[i], pr_sem.at[i], device)
@@ -105,7 +106,8 @@
     own_rope = q_hbm.at[:, pl.ds(latent, ROPE_DIM), :]
     own = [pltpu.make_async_copy(q_hbm.at[:, pl.ds(0, latent), :], q_raw, own_sem.at[0]),
            pltpu.make_async_copy(own_rope, rope_raw.at[me], own_sem.at[1])]
-    for copy in own:
+    lengths = pltpu.make_async_copy(len_hbm, len_ref, len_sem)
+    for copy in own + [lengths]:
         copy.start()
     for step in range(SLOTS - 1):
         fetch(step).start()
@@ -191,6 +193,7 @@
     lax.fori_loop(0, rows // heads, place_rope, 0)
     got_across(0).wait_recv()
     relay(0).start()
+    lengths.wait()
 
     def chunk_step(g, carry):
         @pl.when(g + 1 < num_chunks)
@@ -222,8 +225,10 @@
             return lse_acc
 
         lse_acc = lax.fori_loop(0, per_chunk, pair_step, jnp.zeros((GROUP * heads, 128), jnp.float32))
-        padded = jnp.concatenate([lse_acc, jnp.zeros((128 - GROUP * heads, 128), jnp.float32)], axis=0)
-        lse_buf[g] = padded.T[:CHUNK]
+        columns = jnp.concatenate([lse_acc, lse_acc], axis=0).T
+        half = CHUNK // 2
+        left = lax.broadcasted_iota(jnp.int32, (half, 128), 1) < GROUP * heads
+        lse_buf[g] = jnp.where(left, columns[:half], columns[half:CHUNK])
 
         @pl.when(g < 2 * quarter)
         def _():
@@ -242,42 +247,53 @@
 
     own_first = (2 + core) * quarter
 
+    def drain(k, carry):
+        send_across(k).wait_send()
+        send_sibling(k).wait_send()
+        relay(k).wait_send()
+        return carry
+
+    lax.fori_loop(0, num_chunks, drain, 0)
+    send_rope(0, own_rope, me, across).wait_send()
+    send_rope(1, own_rope, me, sibling).wait_send()
+    send_rope(2, rope_raw.at[across], across, sibling).wait_send()
+
+    def sent(k):
+        for slot in range(GROUP - 1):
+            for copy in send_part(k, slot, sibling):
+                copy.wait_send()
+
     def merge_step(k, carry):
-        parts_of = [send_part(k, slot, sibling) for slot in range(GROUP - 1)]
-        for part in parts_of:
-            part[0].wait_recv()
+        @pl.when(k > 0)
+        def _():
+            sent(k - 1)
+
+        arriving = [send_part(k, slot, sibling) for slot in range(GROUP - 1)]
+        for copies in arriving:
+            copies[-1].wait_recv()
         lses = [lse_buf[own_first + k]] + [lse_recv[slot, k] for slot in range(GROUP - 1)]
         top = functools.reduce(jnp.maximum, lses)
         total = top + jnp.log(functools.reduce(jnp.add, [jnp.exp(x - top) for x in lses]))
         factors = jnp.concatenate([jnp.exp(x - total) for x in lses], axis=0)
-        padded = jnp.concatenate([factors, jnp.zeros((128 - GROUP * CHUNK, 128), jnp.float32)], axis=0)
-        columns = padded.T[:GROUP * heads]
-        for i in range(CHUNK):
-            if i % PIECE == 0:
-                for part in parts_of:
-                    part[1 + i // PIECE].wait_recv()
-            parts = [o_buf[(own_first + k) * CHUNK + i]] + [o_recv[slot, k, i] for slot in range(GROUP - 1)]
-            merged = functools.reduce(
-                jnp.add, [columns[:, s * CHUNK + i:s * CHUNK + i + 1] * part.astype(jnp.float32) for s, part in enumerate(parts)])
-            out_ref[k * CHUNK + i] = merged.astype(jnp.bfloat16)
+        padded = jnp.concatenate([factors, jnp.zeros((128 - factors.shape[0], 128), jnp.float32)], axis=0)
+        columns = padded.T
+        half = CHUNK // 2
+        i = 0
+        for piece, size in enumerate(PIECES):
+            for copies in arriving:
+                copies[piece].wait_recv()
+            for i in range(i, i + size):
+                factor = columns[i // half * GROUP * heads:(i // half + 1) * GROUP * heads]
+                parts = [o_buf[(own_first + k) * CHUNK + i]] + [o_recv[slot, k, i] for slot in range(GROUP - 1)]
+                merged = functools.reduce(jnp.add, [
+                    factor[:, n * half + i % half:n * half + i % half + 1] * part.astype(jnp.float32)
+                    for n, part in enumerate(parts)])
+                out_ref[k * CHUNK + i] = merged.astype(jnp.bfloat16)
+            i += 1
         return carry
 
     lax.fori_loop(0, quarter, merge_step, 0)
-
-    def drain(k, carry):
-        send_across(k).wait_send()
-        send_sibling(k).wait_send()
-        relay(k).wait_send()
-        return carry
-
-    lax.fori_loop(0, num_chunks, drain, 0)
-    send_rope(0, own_rope, me, across).wait_send()
-    send_rope(1, own_rope, me, sibling).wait_send()
-    send_rope(2, rope_raw.at[across], across, sibling).wait_send()
-    for k in range(quarter):
-        for slot in range(GROUP - 1):
-            for copy in send_part(k, slot, sibling):
-                copy.wait_send()
+    sent(quarter - 1)
 
 
 def solution(mesh):
@@ -294,9 +310,10 @@
             kernel,
             out_shape=pltpu.VMEM((rows // GROUP, GROUP * heads, latent), jnp.bfloat16),
             in_specs=[pl.BlockSpec(memory_space=pl.ANY), pl.BlockSpec(memory_space=pl.ANY),
-                      pl.BlockSpec(memory_space=pltpu.SMEM)],
+                      pl.BlockSpec(memory_space=pl.ANY)],
             out_specs=pl.BlockSpec(memory_space=pltpu.VMEM),
             scratch_shapes=[
+                pltpu.SMEM((rows,), jnp.int32),
                 pltpu.VMEM((heads, latent, rows), jnp.bfloat16),
                 pltpu.VMEM((heads, rows, latent), jnp.bfloat16),
                 pltpu.VMEM((GROUP, rows, heads, latent), jnp.bfloat16),
@@ -306,12 +323,12 @@
                 pltpu.VMEM((SLOTS, PAIR, num_pages, width, page_len), jnp.bfloat16),
                 pltpu.VMEM((rows, GROUP * heads, latent), jnp.bfloat16),
                 pltpu.VMEM((GROUP - 1, quarter, CHUNK, GROUP * heads, latent), jnp.bfloat16),
-                pltpu.VMEM((num_chunks, CHUNK, 128), jnp.float32),
-                pltpu.VMEM((GROUP - 1, quarter, CHUNK, 128), jnp.float32),
-                dma((2,)), dma((3,)), dma((3,)), dma((SLOTS,)),
+                pltpu.VMEM((num_chunks, CHUNK // 2, 128), jnp.float32),
+                pltpu.VMEM((GROUP - 1, quarter, CHUNK // 2, 128), jnp.float32),
+                dma(()), dma((2,)), dma((3,)), dma((3,)), dma((SLOTS,)),
                 dma((num_chunks,)), dma((num_chunks,)), dma((num_chunks,)), dma((num_chunks,)),
                 dma((num_chunks,)), dma((num_chunks,)),
-                dma((GROUP - 1, quarter, CHUNK // PIECE)), dma((GROUP - 1, quarter, CHUNK // PIECE)),
+                dma((GROUP - 1, quarter, len(PIECES))), dma((GROUP - 1, quarter, len(PIECES))),
                 dma((GROUP - 1, quarter)), dma((GROUP - 1, quarter)),
                 pltpu.SemaphoreType.REGULAR,
             ],

time: 148 us -> 147 us (level)
  no operation moved by 1% of the time
where the time goes in v5:
time: 147 us
  Pallas kernels  146 us (99%)
    pallas_call x1, Pallas kernels, local_step(): pl.pallas_call(kernel, out_shape=pltpu.VMEM((rows // GROUP, GROUP * heads...  146 us

profile of v5, /device:TPU:1, one launch (start us, length us, event | category | flops | bytes accessed | tf_op | source)
XLA Modules:
  0.0 147.4 jit_solution(2515671697331410075)
XLA Ops:
  0.0 146.1 %shard_map.37 = bf16[32,64,512]{2,1,0:T(8,128)(2,1)S(1)} custom-call(bf16[16,576,128]{2,1,0:T(8,128)(2,1)} %bitcast.2, bf16[128,4,1,576,256]{4,3,2,1,0:T(8,128)(2,1)} %bitcast.1.cache_hbm, s32[128]{0:T(128)} %len_hbm.1), custom_call_target="tpu_custom_call" | custom-call | tf_op jit(solution)/shard_map/pallas_call | solution.py:309
  146.1 1.3 copy.5

commit v6 on v5

--- a/solution.py
+++ b/solution.py
@@ -12,7 +12,7 @@
 QK_DIM = 192
 GROUP = 4
 CHUNK = 16
-PIECES = (8, 4, 2, 2)
+PIECES = (12, 4)
 PAIR = 2
 SLOTS = 3
 
@@ -38,7 +38,7 @@
     return (mixed / total).astype(jnp.bfloat16), top * scale + jnp.log(total)
 
 
-def kernel(q_hbm, cache_hbm, len_hbm, out_ref, len_ref, q_raw, q_turned, q_all, rope_raw, rope_turned, rope_all, ring, o_buf, o_recv, lse_buf, lse_recv,
+def kernel(q_hbm, cache_hbm, len_hbm, out_ref, len_ref, q_raw, q_turned, q_all, rope_raw, rope_turned, rope_all, ring, o_buf, o_recv, lse_buf, lse_recv, factor_buf,
            len_sem, own_sem, ps_sem, pr_sem, ring_sem, xs_sem, xr_sem, ds_sem, dr_sem, rs_sem, rr_sem, os_sem, or_sem, ls_sem, lr_sem, ready):
     heads, width, rows = q_hbm.shape
     latent = width - ROPE_DIM
@@ -90,18 +90,36 @@
         row = pl.ds(start_row(k), CHUNK)
         return send(q_all.at[across, row], q_all.at[diagonal, row], rs_sem.at[k], rr_sem.at[k], sibling)
 
-    def send_part(g, slot, device):
+    def pieces(last):
+        return PIECES if last else (CHUNK,)
+
+    def send_part(g, slot, device, last):
         k = g % quarter
         copies, begin = [], 0
-        for i, size in enumerate(PIECES):
-            src = o_buf.at[pl.ds(pl.multiple_of(g * CHUNK + begin, size), size)]
+        for i, size in enumerate(pieces(last)):
+            unit = math.gcd(begin, CHUNK)
+            src = o_buf.at[pl.ds(pl.multiple_of(g * CHUNK + begin, unit), size)]
             copies.append(send(src, o_recv.at[slot, k, pl.ds(begin, size)],
                                os_sem.at[slot, k, i], or_sem.at[slot, k, i], device))
             begin += size
-        return copies + [send(lse_buf.at[g], lse_recv.at[slot, k], ls_sem.at[slot, k], lr_sem.at[slot, k], device)]
+        lse = send(lse_buf.at[g], lse_recv.at[slot, k], ls_sem.at[slot, k], lr_sem.at[slot, k], device)
+        return copies[:1] + [lse] + copies[1:]
+
+    def start_part(g, slot, device):
+        for last in (False, True):
+            @pl.when((g % quarter == quarter - 1) == last)
+            def _():
+                for copy in send_part(g, slot, device, last):
+                    copy.start()
 
     def send_rope(i, src, dst, device):
         return send(src, rope_raw.at[dst], ps_sem.at[i], pr_sem.at[i], device)
+
+    def tell(semaphore, device):
+        pl.semaphore_signal(semaphore, inc=1, device_id={"dcp": device}, device_id_type=pl.DeviceIdType.MESH)
+
+    barrier = pltpu.get_barrier_semaphore()
+    tell(barrier, across)
 
     own_rope = q_hbm.at[:, pl.ds(latent, ROPE_DIM), :]
     own = [pltpu.make_async_copy(q_hbm.at[:, pl.ds(0, latent), :], q_raw, own_sem.at[0]),
@@ -112,11 +130,6 @@
     for step in range(SLOTS - 1):
         fetch(step).start()
 
-    def tell(semaphore, device):
-        pl.semaphore_signal(semaphore, inc=1, device_id={"dcp": device}, device_id_type=pl.DeviceIdType.MESH)
-
-    barrier = pltpu.get_barrier_semaphore()
-    tell(barrier, across)
     pl.semaphore_wait(barrier, 3 - 2 * core)
 
     @pl.when(core == 1)
@@ -233,13 +246,11 @@
         @pl.when(g < 2 * quarter)
         def _():
             target = (1 - chip) * 2 + g // quarter
-            for copy in send_part(g, 1 + (g // quarter + core) % 2, target):
-                copy.start()
+            start_part(g, 1 + (g // quarter + core) % 2, target)
 
         @pl.when((g >= 2 * quarter) & (g // quarter - 2 != core))
         def _():
-            for copy in send_part(g, 0, sibling):
-                copy.start()
+            start_part(g, 0, sibling)
 
         return carry
 
@@ -260,40 +271,51 @@
 
     def sent(k):
         for slot in range(GROUP - 1):
-            for copy in send_part(k, slot, sibling):
+            for copy in send_part(k, slot, sibling, k == quarter - 1):
                 copy.wait_send()
 
-    def merge_step(k, carry):
-        @pl.when(k > 0)
-        def _():
-            sent(k - 1)
-
-        arriving = [send_part(k, slot, sibling) for slot in range(GROUP - 1)]
-        for copies in arriving:
-            copies[-1].wait_recv()
+    step = PIECES[-1]
+    half = CHUNK // 2
+    every = GROUP * heads
+
+    def wait_for(k, last, which):
+        for slot in range(GROUP - 1):
+            send_part(k, slot, sibling, last)[which].wait_recv()
+
+    def merge_chunk(k, carry):
+        last = k == quarter - 1
+        wait_for(k, False, 1)
         lses = [lse_buf[own_first + k]] + [lse_recv[slot, k] for slot in range(GROUP - 1)]
         top = functools.reduce(jnp.maximum, lses)
         total = top + jnp.log(functools.reduce(jnp.add, [jnp.exp(x - top) for x in lses]))
         factors = jnp.concatenate([jnp.exp(x - total) for x in lses], axis=0)
         padded = jnp.concatenate([factors, jnp.zeros((128 - factors.shape[0], 128), jnp.float32)], axis=0)
-        columns = padded.T
-        half = CHUNK // 2
-        i = 0
-        for piece, size in enumerate(PIECES):
-            for copies in arriving:
-                copies[piece].wait_recv()
-            for i in range(i, i + size):
-                factor = columns[i // half * GROUP * heads:(i // half + 1) * GROUP * heads]
-                parts = [o_buf[(own_first + k) * CHUNK + i]] + [o_recv[slot, k, i] for slot in range(GROUP - 1)]
+        factor_buf[...] = padded.T
+        for final in (False, True):
+            @pl.when(last == final)
+            def _():
+                wait_for(k, final, 0)
+
+        def merge_piece(m, carry):
+            @pl.when(last & (m == CHUNK // step - 1))
+            def _():
+                wait_for(k, True, 2)
+
+            factor = factor_buf[pl.ds(pl.multiple_of(m * step // half * every, every), every)]
+            factor = jnp.where(m * step % half > 0, pltpu.roll(factor, 128 - step, 1), factor)
+            for i in range(step):
+                row = m * step + i
+                parts = [o_buf[(own_first + k) * CHUNK + row]] + [o_recv[slot, k, row] for slot in range(GROUP - 1)]
                 merged = functools.reduce(jnp.add, [
-                    factor[:, n * half + i % half:n * half + i % half + 1] * part.astype(jnp.float32)
-                    for n, part in enumerate(parts)])
-                out_ref[k * CHUNK + i] = merged.astype(jnp.bfloat16)
-            i += 1
-        return carry
-
-    lax.fori_loop(0, quarter, merge_step, 0)
-    sent(quarter - 1)
+                    factor[:, n * half + i:n * half + i + 1] * part.astype(jnp.float32) for n, part in enumerate(parts)])
+                out_ref[k * CHUNK + row] = merged.astype(jnp.bfloat16)
+            return carry
+
+        return lax.fori_loop(0, CHUNK // step, merge_piece, carry)
+
+    lax.fori_loop(0, quarter, merge_chunk, 0)
+    for k in range(quarter):
+        sent(k)
 
 
 def solution(mesh):
@@ -325,6 +347,7 @@
                 pltpu.VMEM((GROUP - 1, quarter, CHUNK, GROUP * heads, latent), jnp.bfloat16),
                 pltpu.VMEM((num_chunks, CHUNK // 2, 128), jnp.float32),
                 pltpu.VMEM((GROUP - 1, quarter, CHUNK // 2, 128), jnp.float32),
+                pltpu.VMEM((128, 128), jnp.float32),
                 dma(()), dma((2,)), dma((3,)), dma((3,)), dma((SLOTS,)),
                 dma((num_chunks,)), dma((num_chunks,)), dma((num_chunks,)), dma((num_chunks,)),
                 dma((num_chunks,)), dma((num_chunks,)),

time: 147 us -> 146 us (level)
  no operation moved by 1% of the time
where the time goes in v6:
time: 146 us
  Pallas kernels  145 us (99%)
    pallas_call x1, Pallas kernels, local_step(): pl.pallas_call(kernel, out_shape=pltpu.VMEM((rows // GROUP, GROUP * heads...  145 us

profile of v6, /device:TPU:1, one launch (start us, length us, event | category | flops | bytes accessed | tf_op | source)
XLA Modules:
  0.0 146.3 jit_solution(9359586038093833672)
XLA Ops:
  0.0 145.0 %shard_map.37 = bf16[32,64,512]{2,1,0:T(8,128)(2,1)S(1)} custom-call(bf16[16,576,128]{2,1,0:T(8,128)(2,1)} %bitcast.2, bf16[128,4,1,576,256]{4,3,2,1,0:T(8,128)(2,1)} %bitcast.1.cache_hbm, s32[128]{0:T(128)} %len_hbm.1), custom_call_target="tpu_custom_call" | custom-call | tf_op jit(solution)/shard_map/pallas_call | solution.py:331
  145.0 1.3 copy.5

commit v7 on v6

--- a/solution.py
+++ b/solution.py
@@ -39,7 +39,7 @@
 
 
 def kernel(q_hbm, cache_hbm, len_hbm, out_ref, len_ref, q_raw, q_turned, q_all, rope_raw, rope_turned, rope_all, ring, o_buf, o_recv, lse_buf, lse_recv, factor_buf,
-           len_sem, own_sem, ps_sem, pr_sem, ring_sem, xs_sem, xr_sem, ds_sem, dr_sem, rs_sem, rr_sem, os_sem, or_sem, ls_sem, lr_sem, ready):
+           len_sem, own_sem, ps_sem, pr_sem, ring_sem, qs_sem, xr_sem, dr_sem, rr_sem, os_sem, or_sem, ls_sem, lr_sem, ready):
     heads, width, rows = q_hbm.shape
     latent = width - ROPE_DIM
     num_chunks = rows // CHUNK
@@ -66,29 +66,36 @@
         return pltpu.make_async_remote_copy(src_ref=src, dst_ref=dst, send_sem=ssem, recv_sem=rsem,
                                             device_id={"dcp": device}, device_id_type=pl.DeviceIdType.MESH)
 
-    def send_across(k):
-        row = pl.ds(pl.multiple_of((chip * (rows // 2) + k * CHUNK) % rows, CHUNK), CHUNK)
-        return send(q_all.at[me, row], q_all.at[me, row], xs_sem.at[k], xr_sem.at[k], across)
-
-    def got_across(k):
-        row = pl.ds(start_row(k), CHUNK)
-        return send(q_all.at[me, row], q_all.at[across, row], xs_sem.at[k], xr_sem.at[k], across)
-
-    def send_sibling(k):
-        row = pl.ds(start_row(k), CHUNK)
-        return send(q_all.at[me, row], q_all.at[me, row], ds_sem.at[k], dr_sem.at[k], sibling)
-
-    def got_sibling(k):
-        row = pl.ds(start_row(k), CHUNK)
-        return send(q_all.at[me, row], q_all.at[sibling, row], ds_sem.at[k], dr_sem.at[k], sibling)
-
-    def relay(k):
-        row = pl.ds(start_row(k), CHUNK)
-        return send(q_all.at[across, row], q_all.at[across, row], rs_sem.at[k], rr_sem.at[k], sibling)
-
-    def got_relay(k):
-        row = pl.ds(start_row(k), CHUNK)
-        return send(q_all.at[across, row], q_all.at[diagonal, row], rs_sem.at[k], rr_sem.at[k], sibling)
+    groups = [(0, 1)] + [(2**i, 2**i) for i in range(num_chunks.bit_length() - 1)]
+
+    def rows_of(i, begin_at):
+        start, size = groups[i]
+        return pl.ds(pl.multiple_of((begin_at + start * CHUNK) % rows, CHUNK), size * CHUNK)
+
+    def send_across(i):
+        row = rows_of(i, chip * (rows // 2))
+        return send(q_all.at[me, row], q_all.at[me, row], qs_sem, xr_sem.at[i], across)
+
+    def got_across(i):
+        row = rows_of(i, first)
+        return send(q_all.at[me, row], q_all.at[across, row], qs_sem, xr_sem.at[i], across)
+
+    def send_sibling():
+        return send(q_all.at[me], q_all.at[me], qs_sem, dr_sem, sibling)
+
+    def got_sibling():
+        return send(q_all.at[me], q_all.at[sibling], qs_sem, dr_sem, sibling)
+
+    def relay(i):
+        row = rows_of(i, first)
+        return send(q_all.at[across, row], q_all.at[across, row], qs_sem, rr_sem.at[i], sibling)
+
+    def got_relay(i):
+        row = rows_of(i, first)
+        return send(q_all.at[across, row], q_all.at[diagonal, row], qs_sem, rr_sem.at[i], sibling)
+
+    def wait_bytes(ref, semaphore):
+        pltpu.make_async_copy(ref, ref, semaphore).wait()
 
     def pieces(last):
         return PIECES if last else (CHUNK,)
@@ -99,10 +106,9 @@
         for i, size in enumerate(pieces(last)):
             unit = math.gcd(begin, CHUNK)
             src = o_buf.at[pl.ds(pl.multiple_of(g * CHUNK + begin, unit), size)]
-            copies.append(send(src, o_recv.at[slot, k, pl.ds(begin, size)],
-                               os_sem.at[slot, k, i], or_sem.at[slot, k, i], device))
+            copies.append(send(src, o_recv.at[slot, k, pl.ds(begin, size)], os_sem, or_sem.at[k + i], device))
             begin += size
-        lse = send(lse_buf.at[g], lse_recv.at[slot, k], ls_sem.at[slot, k], lr_sem.at[slot, k], device)
+        lse = send(lse_buf.at[g], lse_recv.at[slot, k], ls_sem, lr_sem.at[k], device)
         return copies[:1] + [lse] + copies[1:]
 
     def start_part(g, slot, device):
@@ -113,7 +119,7 @@
                     copy.start()
 
     def send_rope(i, src, dst, device):
-        return send(src, rope_raw.at[dst], ps_sem.at[i], pr_sem.at[i], device)
+        return send(src, rope_raw.at[dst], ps_sem, pr_sem.at[i], device)
 
     def tell(semaphore, device):
         pl.semaphore_signal(semaphore, inc=1, device_id={"dcp": device}, device_id_type=pl.DeviceIdType.MESH)
@@ -169,11 +175,8 @@
 
     lax.fori_loop(0, rows // heads, place, 0)
 
-    def issue_across(k, carry):
-        send_across(k).start()
-        return carry
-
-    lax.fori_loop(0, num_chunks, issue_across, 0)
+    for i in range(len(groups)):
+        send_across(i).start()
 
     @pl.when(core == 1)
     def _():
@@ -181,11 +184,7 @@
 
     send_rope(1, own_rope, me, sibling).start()
 
-    def issue_sibling(k, carry):
-        send_sibling(k).start()
-        return carry
-
-    lax.fori_loop(0, num_chunks, issue_sibling, 0)
+    send_sibling().start()
     send_rope(0, own_rope, across, across).wait_recv()
     send_rope(2, rope_raw.at[across], across, sibling).start()
     own[1].wait()
@@ -207,15 +206,19 @@
     got_across(0).wait_recv()
     relay(0).start()
     lengths.wait()
+    got_sibling().wait_recv()
 
     def chunk_step(g, carry):
-        @pl.when(g + 1 < num_chunks)
-        def _():
-            got_across(g + 1).wait_recv()
-            relay(g + 1).start()
-
-        got_sibling(g).wait_recv()
-        got_relay(g).wait_recv()
+        for i, (start, _) in enumerate(groups):
+            if i > 0:
+                @pl.when(g + 1 == start)
+                def _():
+                    got_across(i).wait_recv()
+                    relay(i).start()
+
+            @pl.when(g == start)
+            def _():
+                got_relay(i).wait_recv()
 
         def pair_step(p, lse_acc):
             step = g * per_chunk + p
@@ -258,33 +261,20 @@
 
     own_first = (2 + core) * quarter
 
-    def drain(k, carry):
-        send_across(k).wait_send()
-        send_sibling(k).wait_send()
-        relay(k).wait_send()
-        return carry
-
-    lax.fori_loop(0, num_chunks, drain, 0)
-    send_rope(0, own_rope, me, across).wait_send()
-    send_rope(1, own_rope, me, sibling).wait_send()
-    send_rope(2, rope_raw.at[across], across, sibling).wait_send()
-
-    def sent(k):
-        for slot in range(GROUP - 1):
-            for copy in send_part(k, slot, sibling, k == quarter - 1):
-                copy.wait_send()
+    wait_bytes(q_all.at[pl.ds(0, GROUP - 1)], qs_sem)
+    wait_bytes(rope_raw.at[pl.ds(0, GROUP - 1)], ps_sem)
 
     step = PIECES[-1]
     half = CHUNK // 2
     every = GROUP * heads
 
-    def wait_for(k, last, which):
-        for slot in range(GROUP - 1):
-            send_part(k, slot, sibling, last)[which].wait_recv()
+    def wait_for(k, last, i):
+        begin = sum(pieces(last)[:i])
+        wait_bytes(o_recv.at[:, k, pl.ds(begin, pieces(last)[i])], or_sem.at[k + i])
 
     def merge_chunk(k, carry):
         last = k == quarter - 1
-        wait_for(k, False, 1)
+        wait_bytes(lse_recv.at[:, k], lr_sem.at[k])
         lses = [lse_buf[own_first + k]] + [lse_recv[slot, k] for slot in range(GROUP - 1)]
         top = functools.reduce(jnp.maximum, lses)
         total = top + jnp.log(functools.reduce(jnp.add, [jnp.exp(x - top) for x in lses]))
@@ -299,7 +289,7 @@
         def merge_piece(m, carry):
             @pl.when(last & (m == CHUNK // step - 1))
             def _():
-                wait_for(k, True, 2)
+                wait_for(k, True, 1)
 
             factor = factor_buf[pl.ds(pl.multiple_of(m * step // half * every, every), every)]
             factor = jnp.where(m * step % half > 0, pltpu.roll(factor, 128 - step, 1), factor)
@@ -314,8 +304,8 @@
         return lax.fori_loop(0, CHUNK // step, merge_piece, carry)
 
     lax.fori_loop(0, quarter, merge_chunk, 0)
-    for k in range(quarter):
-        sent(k)
+    wait_bytes(o_buf.at[pl.ds(0, (GROUP - 1) * quarter * CHUNK)], os_sem)
+    wait_bytes(lse_buf.at[pl.ds(0, (GROUP - 1) * quarter)], ls_sem)
 
 
 def solution(mesh):
@@ -348,11 +338,9 @@
                 pltpu.VMEM((num_chunks, CHUNK // 2, 128), jnp.float32),
                 pltpu.VMEM((GROUP - 1, quarter, CHUNK // 2, 128), jnp.float32),
                 pltpu.VMEM((128, 128), jnp.float32),
-                dma(()), dma((2,)), dma((3,)), dma((3,)), dma((SLOTS,)),
-                dma((num_chunks,)), dma((num_chunks,)), dma((num_chunks,)), dma((num_chunks,)),
-                dma((num_chunks,)), dma((num_chunks,)),
-                dma((GROUP - 1, quarter, len(PIECES))), dma((GROUP - 1, quarter, len(PIECES))),
-                dma((GROUP - 1, quarter)), dma((GROUP - 1, quarter)),
+                dma(()), dma((2,)), dma(()), dma((3,)), dma((SLOTS,)),
+                dma(()), dma((num_chunks.bit_length(),)), dma(()), dma((num_chunks.bit_length(),)),
+                dma(()), dma((quarter + len(PIECES) - 1,)), dma(()), dma((quarter,)),
                 pltpu.SemaphoreType.REGULAR,
             ],
             compiler_params=pltpu.CompilerParams(collective_id=0, has_side_effects=True, vmem_limit_bytes=60 * 2**20),

time: 146 us -> 146 us (level)
  no operation moved by 1% of the time
where the time goes in v7:
time: 146 us
  Pallas kernels  144 us (99%)
    pallas_call x1, Pallas kernels, local_step(): pl.pallas_call(kernel, out_shape=pltpu.VMEM((rows // GROUP, GROUP * heads...  144 us

profile of v7, /device:TPU:1, one launch (start us, length us, event | category | flops | bytes accessed | tf_op | source)
XLA Modules:
  0.0 145.7 jit_solution(5314339434774174724)
XLA Ops:
  0.0 144.4 %shard_map.37 = bf16[32,64,512]{2,1,0:T(8,128)(2,1)S(1)} custom-call(bf16[16,576,128]{2,1,0:T(8,128)(2,1)} %bitcast.2, bf16[128,4,1,576,256]{4,3,2,1,0:T(8,128)(2,1)} %bitcast.1.cache_hbm, s32[128]{0:T(128)} %len_hbm.1), custom_call_target="tpu_custom_call" | custom-call | tf_op jit(solution)/shard_map/pallas_call | solution.py:321
  144.4 1.3 copy.5

commit v8 on v7

--- a/solution.py
+++ b/solution.py
@@ -14,6 +14,7 @@
 CHUNK = 16
 PIECES = (12, 4)
 PAIR = 2
+SIBLING = 0
 SLOTS = 3
 
 
@@ -38,8 +39,27 @@
     return (mixed / total).astype(jnp.bfloat16), top * scale + jnp.log(total)
 
 
-def kernel(q_hbm, cache_hbm, len_hbm, out_ref, len_ref, q_raw, q_turned, q_all, rope_raw, rope_turned, rope_all, ring, o_buf, o_recv, lse_buf, lse_recv, factor_buf,
-           len_sem, own_sem, ps_sem, pr_sem, ring_sem, qs_sem, xr_sem, dr_sem, rr_sem, os_sem, or_sem, ls_sem, lr_sem, ready):
+def mix(factor, parts, i, first=0):
+    half = CHUNK // 2
+    return functools.reduce(jnp.add, [
+        factor[:, n * half + i:n * half + i + 1] * part.astype(jnp.float32) for n, part in enumerate(parts, first)])
+
+
+def store(early, tail, base, factor, out_hbm, buf, sems):
+    done = early.shape[0]
+    copies = [pltpu.make_async_copy(early, out_hbm.at[pl.ds(0, done)], sems.at[0]),
+              pltpu.make_async_copy(buf, out_hbm.at[pl.ds(done, buf.shape[0])], sems.at[1])]
+    copies[0].start()
+    for i in range(buf.shape[0]):
+        merged = base[i] + mix(factor[...], [tail[0, i]], i, 2) + mix(factor[...], [tail[1, i]], i, 3)
+        buf[i] = merged.astype(jnp.bfloat16)
+    copies[1].start()
+    for copy in copies:
+        copy.wait()
+
+
+def kernel(q_hbm, cache_hbm, len_hbm, out_ref, tail_ref, base_ref, tail_factor, len_ref, q_raw, q_turned, q_all, rope_raw, rope_turned, rope_all, ring, o_buf, o_recv, lse_buf, lse_recv, factor_buf, stage,
+           len_sem, own_sem, ps_sem, pr_sem, ring_sem, qs_sem, xr_sem, dr_sem, rr_sem, os_sem, or_sem, ls_sem, lr_sem, hs_sem, hr_sem, ready):
     heads, width, rows = q_hbm.shape
     latent = width - ROPE_DIM
     num_chunks = rows // CHUNK
@@ -97,26 +117,49 @@
     def wait_bytes(ref, semaphore):
         pltpu.make_async_copy(ref, ref, semaphore).wait()
 
-    def pieces(last):
-        return PIECES if last else (CHUNK,)
+    tail = PIECES[-1]
+    kept = CHUNK - tail
 
     def send_part(g, slot, device, last):
         k = g % quarter
-        copies, begin = [], 0
-        for i, size in enumerate(pieces(last)):
-            unit = math.gcd(begin, CHUNK)
-            src = o_buf.at[pl.ds(pl.multiple_of(g * CHUNK + begin, unit), size)]
-            copies.append(send(src, o_recv.at[slot, k, pl.ds(begin, size)], os_sem, or_sem.at[k + i], device))
-            begin += size
-        lse = send(lse_buf.at[g], lse_recv.at[slot, k], ls_sem, lr_sem.at[k], device)
-        return copies[:1] + [lse] + copies[1:]
+        split = last and slot is not SIBLING
+
+        def part(begin, size, dst, semaphore):
+            src = o_buf.at[pl.ds(pl.multiple_of(g * CHUNK + begin, math.gcd(begin, CHUNK)), size)]
+            return send(src, dst, os_sem, semaphore, device)
+
+        size = kept if split else CHUNK
+        copies = [part(0, size, o_recv.at[slot, k, pl.ds(0, size)], or_sem.at[k]),
+                  send(lse_buf.at[g], lse_recv.at[slot, k], ls_sem, lr_sem.at[k], device)]
+        if split:
+            copies.append(part(kept, tail, tail_ref.at[slot - 1], or_sem.at[quarter]))
+        return copies
+
+    crossing = 2 * quarter
+
+    def hand_over():
+        return send(o_buf.at[pl.ds(crossing * CHUNK - tail, tail)], stage, os_sem, hr_sem, sibling)
+
+    def send_handed():
+        return send(stage, tail_ref.at[1], hs_sem, or_sem.at[quarter], across)
 
     def start_part(g, slot, device):
         for last in (False, True):
             @pl.when((g % quarter == quarter - 1) == last)
             def _():
-                for copy in send_part(g, slot, device, last):
+                copies = send_part(g, slot, device, last)
+                for copy in copies[:2]:
                     copy.start()
+                if len(copies) > 2:
+                    handed = (g == crossing - 1) & (core == 0)
+
+                    @pl.when(handed)
+                    def _():
+                        hand_over().start()
+
+                    @pl.when(jnp.logical_not(handed))
+                    def _():
+                        copies[2].start()
 
     def send_rope(i, src, dst, device):
         return send(src, rope_raw.at[dst], ps_sem, pr_sem.at[i], device)
@@ -219,6 +262,11 @@
             @pl.when(g == start)
             def _():
                 got_relay(i).wait_recv()
+
+        @pl.when((g == crossing + 1) & (core == 1))
+        def _():
+            hand_over().wait_recv()
+            send_handed().start()
 
         def pair_step(p, lse_acc):
             step = g * per_chunk + p
@@ -253,7 +301,7 @@
 
         @pl.when((g >= 2 * quarter) & (g // quarter - 2 != core))
         def _():
-            start_part(g, 0, sibling)
+            start_part(g, SIBLING, sibling)
 
         return carry
 
@@ -264,16 +312,10 @@
     wait_bytes(q_all.at[pl.ds(0, GROUP - 1)], qs_sem)
     wait_bytes(rope_raw.at[pl.ds(0, GROUP - 1)], ps_sem)
 
-    step = PIECES[-1]
     half = CHUNK // 2
     every = GROUP * heads
 
-    def wait_for(k, last, i):
-        begin = sum(pieces(last)[:i])
-        wait_bytes(o_recv.at[:, k, pl.ds(begin, pieces(last)[i])], or_sem.at[k + i])
-
-    def merge_chunk(k, carry):
-        last = k == quarter - 1
+    def factors_of(k):
         wait_bytes(lse_recv.at[:, k], lr_sem.at[k])
         lses = [lse_buf[own_first + k]] + [lse_recv[slot, k] for slot in range(GROUP - 1)]
         top = functools.reduce(jnp.maximum, lses)
@@ -281,31 +323,47 @@
         factors = jnp.concatenate([jnp.exp(x - total) for x in lses], axis=0)
         padded = jnp.concatenate([factors, jnp.zeros((128 - factors.shape[0], 128), jnp.float32)], axis=0)
         factor_buf[...] = padded.T
-        for final in (False, True):
-            @pl.when(last == final)
-            def _():
-                wait_for(k, final, 0)
+
+    def factor_at(m):
+        factor = factor_buf[pl.ds(pl.multiple_of(m * tail // half * every, every), every)]
+        return jnp.where(m * tail % half > 0, pltpu.roll(factor, 128 - tail, 1), factor)
+
+    def merge_chunk(k, carry):
+        last = k == quarter - 1
+        factors_of(k)
+
+        @pl.when(jnp.logical_not(last))
+        def _():
+            wait_bytes(o_buf.at[pl.ds(0, (GROUP - 1) * CHUNK)], or_sem.at[k])
+
+        @pl.when(last)
+        def _():
+            wait_bytes(o_buf.at[pl.ds(0, (GROUP - 1) * CHUNK - 2 * tail)], or_sem.at[k])
 
         def merge_piece(m, carry):
-            @pl.when(last & (m == CHUNK // step - 1))
-            def _():
-                wait_for(k, True, 1)
-
-            factor = factor_buf[pl.ds(pl.multiple_of(m * step // half * every, every), every)]
-            factor = jnp.where(m * step % half > 0, pltpu.roll(factor, 128 - step, 1), factor)
-            for i in range(step):
-                row = m * step + i
+            factor = factor_at(m)
+            for i in range(tail):
+                row = m * tail + i
                 parts = [o_buf[(own_first + k) * CHUNK + row]] + [o_recv[slot, k, row] for slot in range(GROUP - 1)]
-                merged = functools.reduce(jnp.add, [
-                    factor[:, n * half + i:n * half + i + 1] * part.astype(jnp.float32) for n, part in enumerate(parts)])
-                out_ref[k * CHUNK + row] = merged.astype(jnp.bfloat16)
+                out_ref[k * CHUNK + row] = mix(factor, parts, i).astype(jnp.bfloat16)
             return carry
 
-        return lax.fori_loop(0, CHUNK // step, merge_piece, carry)
+        return lax.fori_loop(0, CHUNK // tail - jnp.where(last, 1, 0), merge_piece, carry)
 
     lax.fori_loop(0, quarter, merge_chunk, 0)
+
+    factor = factor_at(CHUNK // tail - 1)
+    tail_factor[...] = factor
+    for i in range(tail):
+        row = kept + i
+        base_ref[i] = mix(factor, [o_buf[(own_first + quarter - 1) * CHUNK + row], o_recv[SIBLING, quarter - 1, row]], i)
+    wait_bytes(tail_ref, or_sem.at[quarter])
     wait_bytes(o_buf.at[pl.ds(0, (GROUP - 1) * quarter * CHUNK)], os_sem)
     wait_bytes(lse_buf.at[pl.ds(0, (GROUP - 1) * quarter)], ls_sem)
+
+    @pl.when(core == 1)
+    def _():
+        send_handed().wait_send()
 
 
 def solution(mesh):
@@ -318,12 +376,15 @@
         quarter = num_chunks // GROUP
         q_blk = jnp.transpose(q_blk, (1, 2, 0))
         dma = pltpu.SemaphoreType.DMA
-        return pl.pallas_call(
+        early_rows = rows // GROUP - PIECES[-1]
+        tile = (GROUP * heads, latent)
+        parts = pl.pallas_call(
             kernel,
-            out_shape=pltpu.VMEM((rows // GROUP, GROUP * heads, latent), jnp.bfloat16),
+            out_shape=(pltpu.VMEM((early_rows, *tile), jnp.bfloat16), pltpu.VMEM((2, PIECES[-1], *tile), jnp.bfloat16),
+                       pltpu.VMEM((PIECES[-1], *tile), jnp.float32), pltpu.VMEM((GROUP * heads, 128), jnp.float32)),
             in_specs=[pl.BlockSpec(memory_space=pl.ANY), pl.BlockSpec(memory_space=pl.ANY),
                       pl.BlockSpec(memory_space=pl.ANY)],
-            out_specs=pl.BlockSpec(memory_space=pltpu.VMEM),
+            out_specs=(pl.BlockSpec(memory_space=pltpu.VMEM),) * 4,
             scratch_shapes=[
                 pltpu.SMEM((rows,), jnp.int32),
                 pltpu.VMEM((heads, latent, rows), jnp.bfloat16),
@@ -338,12 +399,21 @@
                 pltpu.VMEM((num_chunks, CHUNK // 2, 128), jnp.float32),
                 pltpu.VMEM((GROUP - 1, quarter, CHUNK // 2, 128), jnp.float32),
                 pltpu.VMEM((128, 128), jnp.float32),
+                pltpu.VMEM((PIECES[-1], GROUP * heads, latent), jnp.bfloat16),
                 dma(()), dma((2,)), dma(()), dma((3,)), dma((SLOTS,)),
                 dma(()), dma((num_chunks.bit_length(),)), dma(()), dma((num_chunks.bit_length(),)),
-                dma(()), dma((quarter + len(PIECES) - 1,)), dma(()), dma((quarter,)),
+                dma(()), dma((quarter + len(PIECES) - 1,)), dma(()), dma((quarter,)), dma(()), dma(()),
                 pltpu.SemaphoreType.REGULAR,
             ],
             compiler_params=pltpu.CompilerParams(collective_id=0, has_side_effects=True, vmem_limit_bytes=60 * 2**20),
         )(q_blk, cache_blk, len_blk)
+        return pl.pallas_call(
+            store,
+            out_shape=jax.ShapeDtypeStruct((rows // GROUP, *tile), jnp.bfloat16),
+            in_specs=[pl.BlockSpec(memory_space=pltpu.VMEM)] * 4,
+            out_specs=pl.BlockSpec(memory_space=pl.ANY),
+            scratch_shapes=[pltpu.VMEM((PIECES[-1], *tile), jnp.bfloat16), dma((2,))],
+            compiler_params=pltpu.CompilerParams(vmem_limit_bytes=8 * 2**20),
+        )(*[pltpu.with_memory_space_constraint(part, pltpu.VMEM) for part in parts])
 
     return jax.shard_map(local_step, mesh=mesh, in_specs=(P('dp', 'dcp', None), P('dp', None, 'dcp', None, None), P('dp')), out_specs=P(('dp', 'dcp'), None, None), check_vma=False)

time: 146 us -> 145 us (level)
    pallas_call x1 -> x2, Pallas kernels: 144 us -> 145 us  [the longest x1 144 us: local_step(): pl.pallas_call(kernel, out_shape=(pltpu.VMEM((early_rows, *tile), jnp.bfl...]
where the time goes in v8:
time: 145 us
  Pallas kernels  145 us (100%)
    pallas_call x1, Pallas kernels, local_step(): pl.pallas_call(kernel, out_shape=(pltpu.VMEM((early_rows, *tile), jnp.bfl...  144 us

profile of v8, /device:TPU:1, one launch (start us, length us, event | category | flops | bytes accessed | tf_op | source)
XLA Modules:
  0.0 145.4 jit_solution(3124301213281290961)
XLA Ops:
  0.0 144.1 %shard_map.37 = (bf16[28,64,512]{2,1,0:T(8,128)(2,1)S(1)}, bf16[2,4,64,512]{3,2,1,0:T(8,128)(2,1)S(1)}, f32[4,64,512]{2,1,0:T(8,128)S(1)}, f32[64,128]{1,0:T(8,128)S(1)}) custom-call(bf16[16,576,128]{2,1,0:T(8,128)(2,1)} %bitcast.2, bf16[128,4,1,576,256]{4,3,2,1,0:T(8,128)(2,1)} %bitcast.1.cache_hbm, s32[128]{0:T(128)} %len_hbm.1), custom_call_target="tpu_custom_call" | custom-call | tf_op jit(solution)/shard_map/pallas_call | solution.py:381
  144.1 1.3 shard_map.38

commit v9 on v8

--- a/solution.py
+++ b/solution.py
@@ -15,7 +15,7 @@
 PIECES = (12, 4)
 PAIR = 2
 SIBLING = 0
-SLOTS = 3
+SLOTS = 2
 
 
 def attend(q, q_rope, cache, base, length):

time: 145 us -> 148 us (1.021); the launches traced: 145 us -> 145 us
  no operation moved by 1% of the time
where the time goes in v9:
time: 148 us; the launch traced here: 145 us
  Pallas kernels  145 us (98%)
    pallas_call x1, Pallas kernels, local_step(): pl.pallas_call(kernel, out_shape=(pltpu.VMEM((early_rows, *tile), jnp.bfl...  144 us

profile of v9, /device:TPU:1, one launch (start us, length us, event | category | flops | bytes accessed | tf_op | source)
XLA Modules:
  0.0 145.4 jit_solution(15316901519954582224)
XLA Ops:
  0.0 144.1 %shard_map.37 = (bf16[28,64,512]{2,1,0:T(8,128)(2,1)S(1)}, bf16[2,4,64,512]{3,2,1,0:T(8,128)(2,1)S(1)}, f32[4,64,512]{2,1,0:T(8,128)S(1)}, f32[64,128]{1,0:T(8,128)S(1)}) custom-call(bf16[16,576,128]{2,1,0:T(8,128)(2,1)} %bitcast.2, bf16[128,4,1,576,256]{4,3,2,1,0:T(8,128)(2,1)} %bitcast.1.cache_hbm, s32[128]{0:T(128)} %len_hbm.1), custom_call_target="tpu_custom_call" | custom-call | tf_op jit(solution)/shard_map/pallas_call | solution.py:381
  144.1 1.3 shard_map.38
